TPU v7x, 256 devices: a 8x8x2 block of a 8x8x16 slice. The times are simulated.
256 devices in a mesh: rep: 2 (over z), stretch: 2 (over core), tp: 64 (over x, y).
Axes of the slice: x: 8, y: 8, z: 2, core: 2. Of those that a mesh axis runs over, the one named last changes fastest.
The devices are a block of a 8x8x16 slice.
Arguments:
- query: bfloat16 [4, 512, 3072], P(('rep', 'stretch'), 'tp'), parts along dimension 0, may hold values from -64 to 64
- stretch_kv: bfloat16 [2, 4, 512, 3072], P(None, ('rep', 'stretch'), 'tp'), parts along dimension 1, may hold values from -6 to 6
- history_kv: bfloat16 [2, 32768, 3072], P(None, ('rep', 'tp')), parts along dimension 1, may hold values from -6 to 6
- block_mask: int32 [4, 4, 8], P(('rep', 'stretch')), parts along dimension 0, may hold values from 0 to 1, as said below
- noise_level: int32 [4], P(('rep', 'stretch')), parts along dimension 0, may hold values from 0 to 999
- history_blocks: int32 [2], P('rep'), parts along dimension 0, may hold values from 1 to 128
- out_weight: bfloat16 [3072, 6144], P(None, 'tp'), may hold values from -0.109375 to 0.109375
- gate_table: float32 [1000, 6144], P(None, 'tp'), may hold values from -6 to 6
Outputs:
- mixed: bfloat16 [4, 512, 6144], P(('rep', 'stretch'), None, 'tp'), parts along dimension 0
There are 2 independent parts, one for each index of `rep`. A program takes and returns all parts, laid end to end along the dimension named above; an argument that names none is the same for every part. Nothing has to cross between parts.
Inputs may be any that keep to these rules, and one draw needn't show every extreme that they name: block_mask[c, i, 4 + i] = 1 for every query block i; block_mask[0, i, j] = 0 for j < 4.
All inputs are finite; a program needn't handle non-finite values.
Results may differ from a plain program's by a relative error of at most 0.0049.
Values may be sent and summed in bfloat16 or wider, within the bound.
A program may use at most 128 MiB of HBM per device.

v0:
```python
import math

import jax
import jax.numpy as jnp
from jax import lax
from jax.sharding import PartitionSpec as P

H = 24
HD = 128
BLK = 128


NEGATIVE = -1e30


def shifted(value, axis, steps):
    count = lax.axis_size(axis)
    first, last = (max(0, -steps), min(count, count - steps))
    return lax.ppermute(value, axis, [(source, source + steps) for source in range(first, last)])


def head_block(queries, key_rows, value_rows, allowed):
    key_count = key_rows.shape[0]
    head_count = queries.shape[1]
    key_heads = key_rows.reshape(key_count, head_count, HD)
    scores = jnp.einsum("qhd,khd->qhk", queries, key_heads, preferred_element_type=jnp.float32) * (
        1.0 / math.sqrt(HD)
    )
    scores = jnp.where(allowed[:, None, :], scores, NEGATIVE)
    row_peak = jnp.max(scores, axis=2)
    weights = jnp.where(allowed[:, None, :], jnp.exp(scores - row_peak[:, :, None]), 0.0)
    weight_sum = jnp.sum(weights, axis=2)
    output = None
    value_heads = value_rows.reshape(key_count, head_count, HD).astype(jnp.float32)
    output = jnp.einsum("qhk,khd->qhd", weights, value_heads, precision=lax.Precision.HIGHEST)
    return (row_peak, weight_sum, output)


def combine(earlier, later):
    row_peak = jnp.maximum(earlier[0], later[0])
    scale_one = jnp.exp(earlier[0] - row_peak)
    scale_two = jnp.exp(later[0] - row_peak)
    weight_sum = earlier[1] * scale_one + later[1] * scale_two
    output = None
    output = earlier[2] * scale_one[:, :, None] + later[2] * scale_two[:, :, None]
    return (row_peak, weight_sum, output)


def column_table(columns, block_count):
    return (columns[:, None] == jnp.arange(2 * block_count, dtype=jnp.int32)[None, :]).astype(
        jnp.float32
    )


def attend_all(
    queries,
    query_positions,
    fresh_keys,
    fresh_values,
    fresh_hot,
    mask_table,
    history_pair,
    history_live,
    span,
):
    row_count = queries.shape[0]
    head_count = queries.shape[1]
    block_count = mask_table.shape[0]
    query_hot = (
        (query_positions // BLK)[:, None] == jnp.arange(block_count, dtype=jnp.int32)[None, :]
    ).astype(jnp.float32)
    fresh_allowed = jnp.dot(jnp.dot(query_hot, mask_table), fresh_hot.T) > 0.5
    base_peak = jnp.full((row_count, head_count), NEGATIVE, jnp.float32)
    skipped = (
        base_peak,
        jnp.zeros((row_count, head_count), jnp.float32),
        jnp.zeros((row_count, head_count, HD), jnp.float32),
    )
    result = head_block(queries, fresh_keys, fresh_values, fresh_allowed)
    for sub_block in range(history_pair.shape[1] // span):
        lower_row = sub_block * span
        key_rows = history_pair[0, lower_row : lower_row + span]
        value_rows = history_pair[1, lower_row : lower_row + span]
        live_rows = history_live[lower_row : lower_row + span]
        allowed = jnp.broadcast_to(live_rows[None, :], (row_count, span))
        block_part = lax.cond(
            jnp.any(live_rows),
            lambda: head_block(queries, key_rows, value_rows, allowed),
            lambda: skipped,
        )
        result = combine(result, block_part)
    return result


def on_device(
    query, stretch_kv, history_kv, block_mask, noise_level, history_blocks, out_weight, gate_table
):
    tp_count = lax.axis_size("tp")
    tp_index = lax.axis_index("tp")
    local_rows = query.shape[1]
    feature_width = query.shape[2]
    history_rows = history_kv.shape[1]
    block_count = block_mask.shape[1]
    own_pair = stretch_kv[:, 0]
    older_pair = shifted(own_pair, "stretch", 1)
    mask_table = block_mask[0].astype(jnp.float32)
    live_limit = history_blocks[0] * BLK
    fresh_keys = jnp.concatenate([older_pair[0], own_pair[0]], 0)
    fresh_values = jnp.concatenate([older_pair[1], own_pair[1]], 0)
    own_positions = tp_index * local_rows + jnp.arange(local_rows, dtype=jnp.int32)
    fresh_hot = column_table(
        jnp.concatenate([own_positions // BLK, block_count + own_positions // BLK], 0), block_count
    )
    history_positions = tp_index * history_rows + jnp.arange(history_rows, dtype=jnp.int32)
    history_live = history_positions < live_limit
    piece = lax.all_gather(query[0], "tp", axis=0, tiled=True)
    row_count = piece.shape[0]
    positions = jnp.arange(row_count, dtype=jnp.int32)
    row_peak, weight_sum, output = attend_all(
        piece.reshape(row_count, H, HD),
        positions,
        fresh_keys,
        fresh_values,
        fresh_hot,
        mask_table,
        history_kv,
        history_live,
        BLK,
    )
    got_outputs, got_peaks, got_sums = (
        lax.all_to_all(
            output.reshape(tp_count, local_rows, H, HD),
            "tp",
            split_axis=0,
            concat_axis=0,
            tiled=True,
        ),
        lax.all_to_all(
            row_peak.reshape(tp_count, local_rows, H), "tp", split_axis=0, concat_axis=0, tiled=True
        ),
        lax.all_to_all(
            weight_sum.reshape(tp_count, local_rows, H),
            "tp",
            split_axis=0,
            concat_axis=0,
            tiled=True,
        ),
    )
    overall = jnp.max(got_peaks, axis=0)
    factor = jnp.exp(got_peaks - overall[None])
    merged_sum = jnp.sum(got_sums * factor, axis=0)
    merged = jnp.sum(got_outputs * factor[:, :, :, None], axis=0) / merged_sum[:, :, None]
    attended = merged.reshape(local_rows, feature_width).astype(jnp.bfloat16)
    projected = jnp.dot(
        lax.all_gather(attended, "tp", axis=0, tiled=True),
        out_weight,
        preferred_element_type=jnp.float32,
    )
    level_hot = (jnp.arange(gate_table.shape[0], dtype=jnp.int32) == noise_level[0]).astype(
        jnp.float32
    )[None, :]
    gate_row = jnp.dot(level_hot, gate_table, precision=lax.Precision.HIGHEST)
    return (projected * gate_row).astype(jnp.bfloat16)[None]


def solution(mesh):
    return jax.shard_map(
        on_device,
        mesh=mesh,
        in_specs=(
            P(("rep", "stretch"), "tp", None),
            P(None, ("rep", "stretch"), "tp", None),
            P(None, ("rep", "tp"), None),
            P(("rep", "stretch"), None, None),
            P(("rep", "stretch")),
            P("rep"),
            P(None, "tp"),
            P(None, "tp"),
        ),
        out_specs=P(("rep", "stretch"), None, "tp"),
        check_vma=False,
    )
```

profile of v0, /device:TPU:513, one launch (start us, length us, event | category | flops | bytes accessed | tf_op | source)
XLA Modules:
  0.0 530.0 jit_solution(16864020824890484821)
XLA Ops:
  6.6 0.7 all-gather.6.cloned.1.call-update
  7.3 1.3 collective-permute-start
  9.4 1.1 convolution_compare_fusion
  10.4 0.8 slice_bitcast_fusion.3
  11.3 0.6 slice_reduce_fusion.1
  13.1 16.9 %collective-permute-done = bf16[2,8,3072]{2,1,0:T(8,128)(2,1)S(1)} collective-permute-done((bf16[2,8,3072]{2,1,0:T(8,128)(2,1)}, bf16[2,8,3072]{2,1,0:T(8,128)(2,1)S(1)}, u32[]{:S(2)}, u32[]{:S(2)}) %collective-permute-start) | collective-permute-done | bytes 98336 | tf_op jit(solution)/shard_map/ppermute | solution.py:19
  30.0 76.5 %all-gather.6.cloned.1.call-done = bf16[1,512,3072]{2,1,0:T(8,128)(2,1)} async-done(((bf16[1,8,3072]{2,1,0:T(8,128)(2,1)}), bf16[1,512,3072]{2,1,0:T(8,128)(2,1)}) %all-gather.6.cloned.1.call-update) | async-done | bytes 3145744 | tf_op jit(solution)/shard_map/all_gather | solution.py:116
  106.5 4.7 copy.69
  111.2 2.4 fusion.69
  113.6 0.2 fusion.43
  113.8 28.1 %conditional.3 = (f32[512,24]{0,1:T(8,128)}, f32[512,24]{0,1:T(8,128)S(1)}, f32[512,24,128]{0,2,1:T(8,128)}) conditional(s32[]{:T(128)} %convert_element_type.30, () %tuple.23, (pred[128]{0:T(512)(128)(4,1)S(1)}, bf16[2,256,3072]{2,1,0:T(8,128)(2,1)}, bf16[512,24,128]{0,2,1:T(8,128)(2,1)}) %tuple.60), branch_computations={%region_7.8_spmd, %region_8.11_spmd} | conditional | flops 2837422080 | bytes 52101528 | solution.py:86
  113.9 4.7 copy.74
  118.5 1.5 fusion.68
  120.0 4.2 bitcast_reduce_fusion.1
  124.2 2.5 fusion.21
  126.7 8.7 %fusion.28 = f32[512,24,128]{2,0,1:T(8,128)} fusion(bf16[128,24,128]{0,2,1:T(8,128)(2,1)S(1)} %bitcast.90, f32[24,128,512]{2,1,0:T(8,128)S(1)} %get-tuple-element.80, f32[512,24]{0,1:T(8,128)} %get-tuple-element.94, pred[128]{0:T(512)(128)(4,1)S(1)} %get-tuple-element.28), kind=kOutput, calls=%fused_computation.30 | convolution fusion | flops 2422210560 | bytes 13418624 | tf_op jit(solution)/shard_map/cond/branch_1_fun/qhk,khd->qhd/dot_general | solution.py:35
  135.3 6.6 %copy.92 = f32[512,24,128]{0,2,1:T(8,128)} copy(f32[512,24,128]{2,0,1:T(8,128)} %fusion.28) | data formatting | bytes 12582912 | tf_op jit(solution)/shard_map/cond | solution.py:86
  141.9 28.0 %conditional.2 = (f32[512,24]{0,1:T(8,128)}, f32[512,24]{0,1:T(8,128)S(1)}, f32[512,24,128]{0,2,1:T(8,128)}) conditional(s32[]{:T(128)} %convert_element_type.29, () %tuple.21, (pred[128]{0:T(512)(128)(4,1)S(1)}, bf16[2,256,3072]{2,1,0:T(8,128)(2,1)}, bf16[512,24,128]{0,2,1:T(8,128)(2,1)}) %tuple.61), branch_computations={%region_2.3_spmd, %region_3.6_spmd} | conditional | flops 2837422080 | bytes 52101528 | solution.py:86
  141.9 4.6 copy.71
  146.6 1.5 fusion.67
  148.0 4.2 bitcast_reduce_fusion
  152.2 2.5 fusion.4
  154.7 8.7 %fusion.11 = f32[512,24,128]{2,0,1:T(8,128)} fusion(bf16[128,24,128]{0,2,1:T(8,128)(2,1)S(1)} %bitcast.91, f32[24,128,512]{2,1,0:T(8,128)S(1)} %get-tuple-element.76, f32[512,24]{0,1:T(8,128)} %get-tuple-element.100, pred[128]{0:T(512)(128)(4,1)S(1)} %get-tuple-element.25), kind=kOutput, calls=%fused_computation.13 | convolution fusion | flops 2422210560 | bytes 13418624 | tf_op jit(solution)/shard_map/cond/branch_1_fun/qhk,khd->qhd/dot_general | solution.py:35
  163.4 6.5 %copy.90 = f32[512,24,128]{0,2,1:T(8,128)} copy(f32[512,24,128]{2,0,1:T(8,128)} %fusion.11) | data formatting | bytes 12582912 | tf_op jit(solution)/shard_map/cond | solution.py:86
  169.9 0.9 multiply_add_fusion
  170.8 0.1 copy.79
  170.9 0.9 reshape.81
  171.8 10.0 %all-to-all-start.2 = ((f32[64,1,192]{2,1,0:T(1,128)}), f32[64,1,192]{2,1,0:T(1,128)S(1)}, u32[]{:S(2)}, u32[]{:S(2)}) async-start(f32[64,1,192]{2,1,0:T(1,128)} %reshape.81), calls=%async_computation.2 | async-start | bytes 131072 | tf_op jit(solution)/shard_map/all_to_all | solution.py:141
  181.8 0.1 copy.78
  181.9 0.8 reshape.79
  182.8 8.9 %all-to-all-done.2 = f32[64,1,192]{2,1,0:T(1,128)S(1)} async-done(((f32[64,1,192]{2,1,0:T(1,128)}), f32[64,1,192]{2,1,0:T(1,128)S(1)}, u32[]{:S(2)}, u32[]{:S(2)}) %all-to-all-start.2) | async-done | bytes 49184 | tf_op jit(solution)/shard_map/all_to_all | solution.py:141
  191.7 6.7 %all-to-all-start.1 = ((f32[64,1,192]{2,1,0:T(1,128)}), f32[64,1,192]{2,1,0:T(1,128)S(1)}, u32[]{:S(2)}, u32[]{:S(2)}) async-start(f32[64,1,192]{2,1,0:T(1,128)} %reshape.79), calls=%async_computation.1 | async-start | bytes 131072 | tf_op jit(solution)/shard_map/all_to_all | solution.py:138
  198.3 8.6 %fusion.36 = f32[512,24,128]{0,2,1:T(8,128)} fusion(f32[512,24,128]{0,2,1:T(8,128)} %get-tuple-element.62, f32[512,24,128]{0,2,1:T(8,128)} %get-tuple-element.61, f32[512,24]{0,1:T(8,128)S(1)} %get-tuple-element.71, f32[512,24]{0,1:T(8,128)S(1)} %get-tuple-element.70, f32[512,24]{0,1:T(8,128)S(1)} %get-tuple-element.69, ...), kind=kOutput, calls=%fused_computation.37 | convolution fusion | flops 312016896 | bytes 20013056 | tf_op jit(solution)/shard_map/qhk,khd->qhd/dot_general | solution.py:35
  206.9 6.5 %copy.77 = f32[512,24,128]{2,1,0:T(8,128)} copy(f32[512,24,128]{0,2,1:T(8,128)} %fusion.36) | data formatting | bytes 12582912 | tf_op jit(solution)/shard_map/add | solution.py:45
  213.5 13.0 %all-to-all-start = ((f32[64,8,24,128]{3,2,1,0:T(8,128)}), f32[64,8,24,128]{3,2,1,0:T(8,128)}, u32[]{:S(2)}, u32[]{:S(2)}) async-start(f32[64,8,24,128]{3,2,1,0:T(8,128)} %bitcast.87), calls=%async_computation | async-start | bytes 12582912 | tf_op jit(solution)/shard_map/all_to_all | solution.py:131
  226.5 0.5 broadcast.111
  227.1 0.8 reduce
  227.9 0.1 reshape.82
  228.0 0.8 reduce.1
  228.8 0.1 reshape.80
  229.0 0.1 multiply_reduce_fusion.1
  229.1 177.0 %all-to-all-done = f32[64,8,24,128]{3,2,1,0:T(8,128)} async-done(((f32[64,8,24,128]{3,2,1,0:T(8,128)}), f32[64,8,24,128]{3,2,1,0:T(8,128)}, u32[]{:S(2)}, u32[]{:S(2)}) %all-to-all-start) | async-done | bytes 6291488 | tf_op jit(solution)/shard_map/all_to_all | solution.py:131
  406.1 4.4 multiply_reduce_fusion
  410.5 0.1 fusion.55
  410.6 0.6 copy.95
  412.0 0.3 convolution_bitcast_fusion
  412.3 107.2 %all-gather.4.cloned.1.call-done = bf16[512,3072]{1,0:T(8,128)(2,1)} async-done(((bf16[8,3072]{1,0:T(8,128)(2,1)}), bf16[512,3072]{1,0:T(8,128)(2,1)}) %all-gather.4.cloned.1.call-update) | async-done | bytes 3145744 | tf_op jit(solution)/shard_map/all_gather | solution.py:155
  519.5 3.6 fusion.40
  (16 shorter events, 0.3 us)
Async XLA Ops:
  6.5 512.9 %copy-start = (bf16[3072,96]{0,1:T(8,128)(2,1)S(1)}, bf16[3072,96]{0,1:T(8,128)(2,1)}, u32[]{:S(2)}) copy-start(bf16[3072,96]{0,1:T(8,128)(2,1)} %param.18) | copy-start | bytes 1769476
  6.6 99.9 %all-gather.6.cloned.1.call-start = ((), (), s32[]{:S(2)}) async-start(), calls=%async_computation.4 | async-start | bytes 3194880 | tf_op jit(solution)/shard_map/all_gather | solution.py:116
  7.3 22.7 %collective-permute-start = (bf16[2,8,3072]{2,1,0:T(8,128)(2,1)}, bf16[2,8,3072]{2,1,0:T(8,128)(2,1)S(1)}, u32[]{:S(2)}, u32[]{:S(2)}) collective-permute-start(bf16[2,8,3072]{2,1,0:T(8,128)(2,1)} %bitcast.95), channel_id=1, source_target_pairs={{0,64},{1,65},{2,66},{3,67},{4,68},{5,69},{6,70},{7,71},{8,72},{9,... | collective-permute-start | bytes 294920 | tf_op jit(solution)/shard_map/ppermute | solution.py:19
  171.8 19.9 %all-to-all-start.2 = ((f32[64,1,192]{2,1,0:T(1,128)}), f32[64,1,192]{2,1,0:T(1,128)S(1)}, u32[]{:S(2)}, u32[]{:S(2)}) async-start(f32[64,1,192]{2,1,0:T(1,128)} %reshape.81), calls=%async_computation.2 | async-start | bytes 131072 | tf_op jit(solution)/shard_map/all_to_all | solution.py:141
  191.7 21.8 %all-to-all-start.1 = ((f32[64,1,192]{2,1,0:T(1,128)}), f32[64,1,192]{2,1,0:T(1,128)S(1)}, u32[]{:S(2)}, u32[]{:S(2)}) async-start(f32[64,1,192]{2,1,0:T(1,128)} %reshape.79), calls=%async_computation.1 | async-start | bytes 131072 | tf_op jit(solution)/shard_map/all_to_all | solution.py:138
  213.5 192.6 %all-to-all-start = ((f32[64,8,24,128]{3,2,1,0:T(8,128)}), f32[64,8,24,128]{3,2,1,0:T(8,128)}, u32[]{:S(2)}, u32[]{:S(2)}) async-start(f32[64,8,24,128]{3,2,1,0:T(8,128)} %bitcast.87), calls=%async_computation | async-start | bytes 12582912 | tf_op jit(solution)/shard_map/all_to_all | solution.py:131
  226.5 185.5 %copy-start.1 = (f32[1000,96]{0,1:T(8,128)S(1)}, f32[1000,96]{0,1:T(8,128)}, u32[]{:S(2)}) copy-start(f32[1000,96]{0,1:T(8,128)} %param.19) | copy-start | bytes 1152004
  226.5 293.0 %all-gather.4.cloned.1.call-start = ((), (), s32[]{:S(2)}) async-start(), calls=%async_computation.3 | async-start | bytes 3194880 | tf_op jit(solution)/shard_map/all_gather | solution.py:155
Sparse Core Ops, SparseCore 0:
  9.9 96.5 all-gather.5
  411.4 107.9 all-gather.3
where the time goes:
time: 534 us; the launch traced here: 530 us
  waiting for transfers between devices  387 us (72%)
  matrix products  41.7 us (8%)
  local copies, waits for them, and re-layouts  40.8 us (8%)
  starting transfers between devices  31 us (6%)
  between operations  16.1 us (3%)
  other arithmetic  13.1 us (2%)
    all_to_all x1, waiting for transfers between devices, on_device(): lax.all_to_all(output.reshape(tp_count, local_rows, H, HD), 'tp', split_a...  177 us
    all_gather x1, waiting for transfers between devices, on_device(): lax.all_gather(attended, 'tp', axis=0, tiled=True)  107 us
    all_gather x1, waiting for transfers between devices, on_device(): piece = lax.all_gather(query[0], 'tp', axis=0, tiled=True)  76.5 us
    dot_general x3, matrix products, head_block(): jnp.einsum('qhk,khd->qhd', weights, value_heads, precision=lax.Precision....  25.9 us
    ppermute x1, waiting for transfers between devices, shifted(): lax.ppermute(value, axis, [(source, source + steps) for source in range(f...  16.9 us
    cond x2, local copies, waits for them, and re-layouts, attend_all(): lax.cond(jnp.any(live_rows), lambda: head_block(queries, key_rows, value_...  13.1 us
    all_to_all x1, starting transfers between devices, on_device(): lax.all_to_all(output.reshape(tp_count, local_rows, H, HD), 'tp', split_a...  13 us
    dot_general x3, matrix products, head_block(): jnp.einsum('qhd,khd->qhk', queries, key_heads, preferred_element_type=jnp...  10.8 us
  transfers between devices with their start and end apart: 6, of which 5 were waited for; matrix products, arithmetic and copies ran while one was open for 4% of the time, Pallas kernels for 0%

commit v1 on v0

v1 whole, which is shorter than its diff:
```python
import functools
import math

import jax
import jax.numpy as jnp
from jax import lax
from jax.experimental import pallas as pl
from jax.experimental.pallas import tpu as pltpu
from jax.sharding import PartitionSpec as P

HD = 128
BLK = 128
NEGATIVE = -1e30
MESH = pl.DeviceIdType.MESH
F32 = jnp.float32
BF16 = jnp.bfloat16
EXP2_SCALE = math.log2(math.e) / math.sqrt(HD)


def remote(src, dst, send_sem, recv_sem, device):
    return pltpu.make_async_remote_copy(
        src_ref=src,
        dst_ref=dst,
        send_sem=send_sem,
        recv_sem=recv_sem,
        device_id=device,
        device_id_type=MESH,
    )


def dot(left, right, left_dim, right_dim):
    return lax.dot_general(
        left, right, (((left_dim,), (right_dim,)), ((), ())), preferred_element_type=F32
    )


def merged(parts):
    peak = parts[0][0]
    for part_peak, _, _ in parts[1:]:
        peak = jnp.maximum(peak, part_peak)
    total = None
    output = None
    for part_peak, part_sum, part_output in parts:
        weight = part_sum * jnp.exp2((part_peak - peak) * EXP2_SCALE)
        term = part_output.astype(F32) * weight
        total = weight if total is None else total + weight
        output = term if output is None else output + term
    return peak, total, output / total


def kernel(
    side,
    q_hbm,
    s_hbm,
    h_hbm,
    mask_sm,
    noise_sm,
    live_sm,
    w_hbm,
    g_hbm,
    out_ref,
    hist,
    qx,
    fx,
    msend,
    mtab,
    q1,
    q,
    kv,
    frb,
    obuf,
    stats,
    oa,
    oas,
    bbuf,
    ob,
    sb,
    fin,
    gath,
    wt,
    gate,
    loc,
    dds,
    ddr,
    q1s,
    q1r,
    q2s,
    q2r,
    kvs,
    kvr,
    frs,
    frr,
    oss,
    osr,
    sss,
    ssr,
    obs,
    obr,
    sbs,
    sbr,
    g1s,
    g1r,
    g2s,
    g2r,
):
    S = side
    half = S // 2
    R, F = q_hbm.shape
    HR = h_hbm.shape[1]
    T = S * S * R
    FG = F // 8
    HH = FG // HD
    FP = FG // half
    CB = T // half
    GR = math.gcd(FP, HD)
    QB = mask_sm.shape[1]
    NB = mask_sm.shape[2]

    e = lax.axis_index("stretch")
    t = lax.axis_index("tp")
    x = t // S
    y = t % S
    a = x + e * (y - x)
    b = y + e * (x - y)

    def tp_of(a_, b_):
        return (a_ + e * (b_ - a_)) * S + b_ + e * (a_ - b_)

    def at(a_, b_):
        return {"tp": tp_of(a_, b_)}

    other_core = {"stretch": 1 - e}

    def group_of(a_, b_):
        return (a_ % 2) * 4 + (b_ % 2) * 2 + e

    def partner(v):
        return (v + S + 1 - 2 * ((v + e) % 2)) % S

    a2 = partner(a)
    b2 = partner(b)
    block = [(a, b), (a2, b), (a, b2), (a2, b2)]
    ia = a // 2
    jb = b // 2

    ld_hist = pltpu.make_async_copy(h_hbm, hist, loc.at[0])
    ld_q = [
        pltpu.make_async_copy(
            q_hbm.at[:, pl.ds(p * (F // 2), F // 2)], qx.at[p, e], loc.at[1 + p]
        )
        for p in range(2)
    ]
    ld_f = pltpu.make_async_copy(s_hbm, fx.at[:, pl.ds(e * R, R), :], loc.at[3])
    ld_w = pltpu.make_async_copy(w_hbm, wt, loc.at[4])
    ld_g = pltpu.make_async_copy(g_hbm, gate, loc.at[5])
    for copy in ld_q + [ld_f, ld_hist, ld_w, ld_g]:
        copy.start()

    barrier = pltpu.get_barrier_semaphore()
    for k in range(1, S):
        for device in (at((a + k) % S, b), at(a, (b + k) % S)):
            pl.semaphore_signal(barrier, inc=1, device_id=device, device_id_type=MESH)
    for device in (at(a2, b2), other_core):
        pl.semaphore_signal(barrier, inc=1, device_id=device, device_id_type=MESH)

    lane = lax.broadcasted_iota(jnp.int32, (1, T), 1)
    swapped = ((lane // R) % S) * (S * R) + (lane // (S * R)) * R + lane % R
    own_order = jnp.where(e == 0, lane, swapped) // BLK
    other_order = jnp.where(e == 0, swapped, lane) // BLK
    for u in range(NB):
        own_row = jnp.zeros((1, T), F32)
        other_row = jnp.zeros((1, T), F32)
        for i in range(QB):
            bias = (mask_sm[0, i, u].astype(F32) - 1.0) * (-NEGATIVE)
            own_row = jnp.where(own_order == i, bias, own_row)
            other_row = jnp.where(other_order == i, bias, other_row)
        mtab[e, u] = own_row
        msend[u] = other_row

    for copy in ld_q + [ld_f]:
        copy.wait()
    pl.semaphore_wait(barrier, 2 * (S - 1) + 2)

    dq = remote(qx.at[:, e], qx.at[:, e], dds.at[0], ddr.at[0], other_core)
    df = remote(
        fx.at[:, pl.ds(e * R, R), :],
        fx.at[:, pl.ds(e * R, R), :],
        dds.at[1],
        ddr.at[1],
        other_core,
    )
    dm = remote(msend, mtab.at[e], dds.at[2], ddr.at[2], other_core)
    dq.start()
    df.start()
    dm.start()

    def q_cols(b_):
        return pl.ds(pl.multiple_of(((b_ % 2) * 2 + e) * FG, FG), FG)

    q1_rows = pl.ds(pl.multiple_of(b * R, R), R)

    def q1_copy(k):
        b_ = (b + k) % S
        return remote(
            qx.at[:, :, :, q_cols(b_)], q1.at[:, :, q1_rows, :], q1s.at[k], q1r.at[k], at(a, b_)
        )

    q1_own = pltpu.make_async_copy(qx.at[:, :, :, q_cols(b)], q1.at[:, :, q1_rows, :], loc.at[6])

    def kv_cols(p, h):
        start = group_of(*block[p]) * FG + h * HD
        return pl.ds(pl.multiple_of(start, HD), HD)

    def kv_copy(h, p):
        return remote(
            hist.at[:, :, kv_cols(p, h)], kv.at[h, p], kvs.at[h, p], kvr.at[h, p], at(*block[p])
        )

    def kv_own(h):
        return pltpu.make_async_copy(hist.at[:, :, kv_cols(0, h)], kv.at[h, 0], loc.at[8 + h])

    def f_cols(p):
        return pl.ds(pl.multiple_of(group_of(*block[p]) * FG, FG), FG)

    def f_copy(p):
        return remote(
            fx.at[:, :, f_cols(p)],
            frb.at[:, pl.ds(p * 2 * R, 2 * R), :],
            frs.at[p],
            frr.at[p],
            at(*block[p]),
        )

    f_own = pltpu.make_async_copy(
        fx.at[:, :, f_cols(0)], frb.at[:, pl.ds(0, 2 * R), :], loc.at[7]
    )

    q_rows = pl.ds(pl.multiple_of(a * (S * R), S * R), S * R)

    def h_cols(h):
        return pl.ds(pl.multiple_of(h * HD, HD), HD)

    def q2_copy(h, k):
        a_ = (a + k) % S
        return remote(
            q1.at[a_ % 2, :, :, h_cols(h)],
            q.at[h, :, q_rows, :],
            q2s.at[h, k],
            q2r.at[h, k],
            at(a_, b),
        )

    def q2_own(h):
        return pltpu.make_async_copy(
            q1.at[a % 2, :, :, h_cols(h)], q.at[h, :, q_rows, :], loc.at[8 + HH + h]
        )

    dq.wait_recv()
    for k in range(1, S):
        q1_copy(k).start()
    q1_own.start()
    ld_hist.wait()
    for p in (3, 1, 2):
        kv_copy(0, p).start()
    df.wait_recv()
    for p in (3, 1, 2):
        f_copy(p).start()
    for h in range(HH):
        kv_own(h).start()
    f_own.start()
    q1_own.wait()
    for k in range(1, S):
        q1_copy(k).wait_recv()
    for h in range(HH):
        if h > 0:
            for p in (3, 1, 2):
                kv_copy(h, p).start()
        for k in (4, 3, 5, 2, 6, 1, 7) if S == 8 else range(1, S):
            q2_copy(h, k).start()
        q2_own(h).start()

    dm.wait_recv()
    f_own.wait()
    for p in (1, 2, 3):
        f_copy(p).wait_recv()
    live = live_sm[0] * BLK

    def o_copy(h, k):
        i = (ia + k) % half
        return remote(
            obuf.at[h, k], oa.at[h, k], oss.at[h, k], osr.at[h, k], at(2 * i + a % 2, b)
        )

    def os_copy(h, k):
        i = (ia + k) % half
        return remote(
            stats.at[h, k], oas.at[h, k], sss.at[h, k], ssr.at[h, k], at(2 * i + a % 2, b)
        )

    def head(h, carry):
        kv_own(h).wait()
        q2_own(h).wait()
        for p in (1, 2, 3):
            kv_copy(h, p).wait_recv()
        for k in range(1, S):
            q2_copy(h, k).wait_recv()

        def chunk(n, carry):
            k = (n + 1) % half
            cols = pl.ds(pl.multiple_of(((ia + k) % half) * CB, CB), CB)
            queries = jnp.concatenate([q[h, 0, cols, :], q[h, 1, cols, :]], axis=0)
            scores = []
            for p in range(4):
                first = tp_of(*block[p]) * HR
                part = dot(kv[h, p, 0], queries, 1, 1)
                for r in range(HR // BLK):
                    bias = jnp.where(first + r * BLK < live, 0.0, NEGATIVE)
                    scores.append(part[r * BLK : (r + 1) * BLK] + bias)
            fresh_bias = []
            for p in range(4):
                u = (tp_of(*block[p]) * R) // BLK
                older = mtab[1, u, :, cols]
                own0 = mtab[0, QB + u, :, cols]
                own1 = mtab[1, QB + u, :, cols]
                none = jnp.full((1, CB), NEGATIVE, F32)
                for left, right in ((own0, older), (none, own1)):
                    row = jnp.concatenate([left, right], axis=1)
                    fresh_bias.append(jnp.broadcast_to(row, (R, 2 * CB)))
            fresh = dot(frb[0, :, h_cols(h)], queries, 1, 1) + jnp.concatenate(fresh_bias, axis=0)
            peak = jnp.max(fresh, axis=0, keepdims=True)
            for part in scores:
                peak = jnp.maximum(peak, jnp.max(part, axis=0, keepdims=True))
            weights = jnp.exp2((fresh - peak) * EXP2_SCALE)
            total = jnp.sum(weights, axis=0, keepdims=True)
            output = dot(frb[1, :, h_cols(h)], weights.astype(BF16), 0, 0)
            per = HR // BLK
            for p in range(4):
                block_weights = []
                for part in scores[p * per : (p + 1) * per]:
                    weights = jnp.exp2((part - peak) * EXP2_SCALE)
                    total = total + jnp.sum(weights, axis=0, keepdims=True)
                    block_weights.append(weights.astype(BF16))
                output = output + dot(
                    kv[h, p, 1], jnp.concatenate(block_weights, axis=0), 0, 0
                )
            output = (output / total).astype(BF16)
            obuf[h, k, 0] = output[:, :CB]
            obuf[h, k, 1] = output[:, CB:]
            stats[h, k] = jnp.concatenate(
                [peak[:, :CB], total[:, :CB], peak[:, CB:], total[:, CB:], jnp.zeros((4, CB), F32)],
                axis=0,
            )

            @pl.when(n >= 1)
            def _():
                o_copy(h, n).start()
                os_copy(h, n).start()

            return carry

        return lax.fori_loop(0, half, chunk, carry)

    lax.fori_loop(0, HH, head, 0)

    for h in range(HH):
        for k in range(1, half):
            o_copy(h, k).wait_recv()
            os_copy(h, k).wait_recv()
        for c in range(2):
            rows = slice(2 * c, 2 * c + 1)
            sums = slice(2 * c + 1, 2 * c + 2)
            parts = [(stats[h, 0, rows], stats[h, 0, sums], obuf[h, 0, c])]
            for k in range(1, half):
                parts.append((oas[h, k, rows], oas[h, k, sums], oa[h, k, c]))
            peak, total, output = merged(parts)
            bbuf[c, h * HD : (h + 1) * HD, :] = output.astype(BF16)
            row = (c * HH + h) * 2
            sb[0, row] = peak
            sb[0, row + 1] = total

    def b_copy(k):
        j = (jb + k) % half
        return remote(
            bbuf.at[:, pl.ds(pl.multiple_of(j * FP, GR), FP), :],
            ob.at[k],
            obs.at[k],
            obr.at[k],
            at(a, 2 * j + b % 2),
        )

    def bs_copy(k):
        j = (jb + k) % half
        return remote(sb.at[0], sb.at[k], sbs.at[k], sbr.at[k], at(a, 2 * j + b % 2))

    for k in range(1, half):
        bs_copy(k).start()
        b_copy(k).start()
    for k in range(1, half):
        bs_copy(k).wait_recv()
        b_copy(k).wait_recv()
    for c in range(2):
        for p in range(FP // GR):
            first = pl.multiple_of(jb * FP + p * GR, GR)
            row = (c * HH + first // HD) * 2
            parts = []
            for k in range(half):
                piece = (
                    bbuf[c, pl.ds(first, GR), :]
                    if k == 0
                    else ob[k, c, p * GR : (p + 1) * GR, :]
                )
                parts.append((sb[k, row], sb[k, row + 1], piece))
            _, _, output = merged(parts)
            fin[c, p * GR : (p + 1) * GR, :] = output.astype(BF16)

    gd = remote(fin.at[1 - e], gath.at[1, a, b], dds.at[3], ddr.at[3], other_core)
    gd.start()
    g_own = pltpu.make_async_copy(fin.at[e], gath.at[0, a, b], loc.at[8 + 2 * HH])
    g_own.start()

    def g1_copy(kind, k):
        dst = gath.at[0, a, b] if kind == 0 else gath.at[1, b, a]
        src = fin.at[e] if kind == 0 else gath.at[1, b, a]
        return remote(src, dst, g1s.at[kind, k], g1r.at[kind, k], at((a + k) % S, b))

    for k in range(1, S):
        g1_copy(0, k).start()
    gd.wait_recv()
    for k in range(1, S):
        g1_copy(1, k).start()
    g_own.wait()

    def g2_copy(d, s, kind):
        sign = 1 - 2 * d
        source = (b + S - sign * (s - 1)) % S
        slab = gath.at[0, :, source] if kind == 0 else gath.at[1, source]
        return remote(
            slab, slab, g2s.at[d, s, kind], g2r.at[d, s, kind], at(a, (b + S + sign) % S)
        )

    sent = []
    for s in range(1, half + 1):
        for kind in range(2):
            if s == 1:
                for k in range(1, S):
                    g1_copy(kind, k).wait_recv()
            for d in range(2):
                if s == half and kind != d:
                    continue
                if s > 1:
                    g2_copy(d, s - 1, kind).wait_recv()
                g2_copy(d, s, kind).start()
                sent.append((d, s, kind))
    for d in range(2):
        g2_copy(d, half - 1, 1 - d).wait_recv()
        g2_copy(d, half, d).wait_recv()

    ld_w.wait()
    ld_g.wait()
    results = []
    for kind in range(2):
        e_kind = e if kind == 0 else 1 - e
        result = None
        for pa in range(2):
            for pb in range(2):
                group = pa * 4 + pb * 2 + e_kind
                weight = wt[:, pl.ds(pl.multiple_of(group * FG, FG), FG)]
                rows = jnp.concatenate(
                    [
                        jnp.concatenate(
                            [gath[kind, 2 * i + pa, 2 * j + pb] for j in range(half)], axis=0
                        )
                        for i in range(half)
                    ],
                    axis=1,
                )
                term = dot(weight, rows, 1, 0)
                result = term if result is None else result + term
        results.append(result)
    natural = jnp.where(e == 0, results[0], results[1])
    crossed = jnp.where(e == 0, results[1], results[0])
    width = natural.shape[0]
    lanes = -(-width // 128) * 128
    if lanes > width:
        crossed = jnp.concatenate([crossed, jnp.zeros((lanes - width, T), F32)], axis=0)
    crossed = crossed.T
    crossed = jnp.concatenate(
        [
            crossed[(m * S + n) * R : (m * S + n + 1) * R]
            for n in range(S)
            for m in range(S)
        ],
        axis=0,
    )
    crossed = crossed.T[:width]
    levels = lax.broadcasted_iota(jnp.int32, gate.shape, 1)
    gate_column = jnp.sum(jnp.where(levels == noise_sm[0], gate[...], 0.0), axis=1, keepdims=True)
    out_ref[...] = ((natural + crossed) * gate_column).astype(BF16)

    for copy in (dq, df, dm, gd):
        copy.wait_send()
    for k in range(1, S):
        q1_copy(k).wait_send()
        g1_copy(0, k).wait_send()
        g1_copy(1, k).wait_send()
    for p in (1, 2, 3):
        f_copy(p).wait_send()
    for h in range(HH):
        for p in (1, 2, 3):
            kv_copy(h, p).wait_send()
        for k in range(1, S):
            q2_copy(h, k).wait_send()
        for k in range(1, half):
            o_copy(h, k).wait_send()
            os_copy(h, k).wait_send()
    for k in range(1, half):
        b_copy(k).wait_send()
        bs_copy(k).wait_send()
    for key in sent:
        g2_copy(*key).wait_send()


def on_device(
    side, query, stretch_kv, history_kv, block_mask, noise_level, history_blocks, out_weight, gate_table
):
    S = side
    half = S // 2
    R, F = query.shape[1:]
    HR = history_kv.shape[1]
    T = S * S * R
    FG = F // 8
    HH = FG // HD
    FP = FG // half
    CB = T // half
    C = out_weight.shape[1]
    DMA = pltpu.SemaphoreType.DMA
    any_space = pl.BlockSpec(memory_space=pl.ANY)
    smem = pl.BlockSpec(memory_space=pltpu.SMEM)
    out = pl.pallas_call(
        functools.partial(kernel, side),
        out_shape=jax.ShapeDtypeStruct((C, T), BF16),
        in_specs=[any_space, any_space, any_space, smem, smem, smem, any_space, any_space],
        out_specs=pl.BlockSpec(memory_space=pltpu.VMEM),
        scratch_shapes=[
            pltpu.VMEM((2, HR, F), BF16),
            pltpu.VMEM((2, 2, R, F // 2), BF16),
            pltpu.VMEM((2, 2 * R, F), BF16),
            pltpu.VMEM((block_mask.shape[2], 1, T), F32),
            pltpu.VMEM((2, block_mask.shape[2], 1, T), F32),
            pltpu.VMEM((2, 2, S * R, FG), BF16),
            pltpu.VMEM((HH, 2, T, HD), BF16),
            pltpu.VMEM((HH, 4, 2, HR, HD), BF16),
            pltpu.VMEM((2, 8 * R, FG), BF16),
            pltpu.VMEM((HH, half, 2, HD, CB), BF16),
            pltpu.VMEM((HH, half, 8, CB), F32),
            pltpu.VMEM((HH, half, 2, HD, CB), BF16),
            pltpu.VMEM((HH, half, 8, CB), F32),
            pltpu.VMEM((2, FG, CB), BF16),
            pltpu.VMEM((half, 2, FP, CB), BF16),
            pltpu.VMEM((half, 4 * HH, 1, CB), F32),
            pltpu.VMEM((2, FP, CB), BF16),
            pltpu.VMEM((2, S, S, FP, CB), BF16),
            pltpu.VMEM((C, F), BF16),
            pltpu.VMEM((C, gate_table.shape[0]), F32),
            DMA((9 + 2 * HH,)),
            DMA((4,)),
            DMA((4,)),
            DMA((S,)),
            DMA((S,)),
            DMA((HH, S)),
            DMA((HH, S)),
            DMA((HH, 4)),
            DMA((HH, 4)),
            DMA((4,)),
            DMA((4,)),
            DMA((HH, half)),
            DMA((HH, half)),
            DMA((HH, half)),
            DMA((HH, half)),
            DMA((half,)),
            DMA((half,)),
            DMA((half,)),
            DMA((half,)),
            DMA((2, S)),
            DMA((2, S)),
            DMA((2, half + 1, 2)),
            DMA((2, half + 1, 2)),
        ],
        compiler_params=pltpu.CompilerParams(
            collective_id=0, has_side_effects=True, vmem_limit_bytes=48 * 1024 * 1024
        ),
    )(
        query[0],
        stretch_kv[:, 0],
        history_kv,
        block_mask,
        noise_level,
        history_blocks,
        out_weight.T,
        gate_table.T,
    )
    return out.T[None]


def solution(mesh):
    side = math.isqrt(mesh.shape["tp"])
    return jax.shard_map(
        functools.partial(on_device, side),
        mesh=mesh,
        in_specs=(
            P(("rep", "stretch"), "tp", None),
            P(None, ("rep", "stretch"), "tp", None),
            P(None, ("rep", "tp"), None),
            P(("rep", "stretch"), None, None),
            P(("rep", "stretch")),
            P("rep"),
            P(None, "tp"),
            P(None, "tp"),
        ),
        out_specs=P(("rep", "stretch"), None, "tp"),
        check_vma=False,
    )
```

time: 534 us -> 105 us (0.20)
  waiting for transfers between devices: 387 us -> 0 us
  Pallas kernels: 0 us -> 96.4 us
  matrix products: 41.7 us -> 0 us
  local copies, waits for them, and re-layouts: 40.8 us -> 6.96 us
  starting transfers between devices: 31 us -> 0 us
  between operations: 16.1 us -> 1.32 us
  other arithmetic: 13.1 us -> 0 us
    all_to_all x3 -> x0, waiting for transfers between devices: 186 us -> none  [the longest x1 177 us: on_device(): lax.all_to_all(output.reshape(tp_count, local_rows, H, HD), 'tp', split_a...]
    all_gather x2 -> x0, waiting for transfers between devices: 184 us -> none  [the longest x1 107 us: on_device(): lax.all_gather(attended, 'tp', axis=0, tiled=True)]
    pallas_call x0 -> x1, Pallas kernels: none -> 96.4 us  [on_device(): pl.pallas_call(functools.partial(kernel, side), out_shape=jax.ShapeDtypeS...]
    dot_general x9 -> x0, matrix products: 41.7 us -> none  [the longest x3 25.9 us: head_block(): jnp.einsum('qhk,khd->qhd', weights, value_heads, precision=lax.Precision....]
    all_to_all x3 -> x0, starting transfers between devices: 29.7 us -> none  [the longest x1 13 us: on_device(): lax.all_to_all(output.reshape(tp_count, local_rows, H, HD), 'tp', split_a...]
    ppermute x1 -> x0, waiting for transfers between devices: 16.9 us -> none  [shifted(): lax.ppermute(value, axis, [(source, source + steps) for source in range(f...]
    cond x2 -> x0, local copies, waits for them, and re-layouts: 13.1 us -> none  [attend_all(): lax.cond(jnp.any(live_rows), lambda: head_block(queries, key_rows, value_...]
    reduce_sum x5 -> x0, other arithmetic: 9.7 us -> none  [the longest x3 5.21 us: head_block(): weight_sum = jnp.sum(weights, axis=2)]
  transfers between devices with their start and end apart: 6 -> 0, of which waited for: 5 -> 0; matrix products, arithmetic and copies ran while one was open for 4% -> 0% of each run, Pallas kernels for 0% -> 0%
where the time goes in v1:
time: 105 us
  Pallas kernels  96.4 us (92%)
  local copies, waits for them, and re-layouts  6.96 us (7%)
  between operations  1.32 us (1%)
    pallas_call x1, Pallas kernels, on_device(): pl.pallas_call(functools.partial(kernel, side), out_shape=jax.ShapeDtypeS...  96.4 us
    unnamed x13, local copies, waits for them, and re-layouts  6.96 us

profile of v1, /device:TPU:513, one launch (start us, length us, event | category | flops | bytes accessed | tf_op | source)
XLA Modules:
  0.0 104.6 jit_solution(13772544106121506772)
XLA Ops:
  1.3 0.0 copy-start
  1.3 1.9 %copy-done = bf16[2,256,3072]{2,1,0:T(8,128)(2,1)S(1)} copy-done((bf16[2,256,3072]{2,1,0:T(8,128)(2,1)S(1)}, bf16[2,256,3072]{2,1,0:T(8,128)(2,1)}, u32[]{:S(2)}) %copy-start) | copy-done | bytes 3145752
  3.2 0.0 copy-start.1
  3.2 1.1 %copy-done.1 = bf16[3072,96]{0,1:T(8,128)(2,1)S(1)} copy-done((bf16[3072,96]{0,1:T(8,128)(2,1)S(1)}, bf16[3072,96]{0,1:T(8,128)(2,1)}, u32[]{:S(2)}) %copy-start.1) | copy-done | bytes 589848
  4.3 0.0 copy-start.2
  4.3 1.0 copy-done.2
  5.2 0.0 copy-start.3
  5.3 0.9 copy-done.3
  6.1 0.0 copy-start.4
  6.1 0.8 copy-done.4
  6.9 0.0 copy-start.5
  6.9 0.7 copy-done.5
  7.6 96.4 %shard_map.82 = bf16[96,512]{1,0:T(8,128)(2,1)S(1)} custom-call(bf16[8,3072]{1,0:T(8,128)(2,1)S(1)} %bitcast.11, bf16[2,8,3072]{2,1,0:T(8,128)(2,1)S(1)} %bitcast.10, bf16[2,256,3072]{2,1,0:T(8,128)(2,1)S(1)} %copy-done, s32[1,4,8]{2,1,0:T(4,128)S(1)} %copy-done.5, s32[1]{0:T(128)S(6)} %copy.10.noise_sm, s32[1]{0:T(128)S(6)} %copy.11.live_sm, ...), custom_call_target="tpu_custom_call" | custom-call | tf_op jit(solution)/shard_map/pallas_call | solution.py:539
  104.0 0.6 copy.12
Async XLA Ops:
  1.3 1.9 %copy-start = (bf16[2,256,3072]{2,1,0:T(8,128)(2,1)S(1)}, bf16[2,256,3072]{2,1,0:T(8,128)(2,1)}, u32[]{:S(2)}) copy-start(bf16[2,256,3072]{2,1,0:T(8,128)(2,1)} %h_hbm.1) | copy-start | bytes 9437188
  3.2 1.1 %copy-start.1 = (bf16[3072,96]{0,1:T(8,128)(2,1)S(1)}, bf16[3072,96]{0,1:T(8,128)(2,1)}, u32[]{:S(2)}) copy-start(bf16[3072,96]{0,1:T(8,128)(2,1)} %param.14) | copy-start | bytes 1769476
  4.3 1.0 copy-start.2
  5.2 0.9 copy-start.3
  6.1 0.8 copy-start.4
  6.9 0.7 copy-start.5

commit v2 on v1

--- a/solution.py
+++ b/solution.py
@@ -14,6 +14,8 @@
 MESH = pl.DeviceIdType.MESH
 F32 = jnp.float32
 BF16 = jnp.bfloat16
+SMALL = 1e-30
+STEP = 4
 EXP2_SCALE = math.log2(math.e) / math.sqrt(HD)
 
 
@@ -45,7 +47,7 @@
         term = part_output.astype(F32) * weight
         total = weight if total is None else total + weight
         output = term if output is None else output + term
-    return peak, total, output / total
+    return peak, total, output / jnp.maximum(total, SMALL)
 
 
 def kernel(
@@ -53,9 +55,9 @@
     q_hbm,
     s_hbm,
     h_hbm,
-    mask_sm,
-    noise_sm,
-    live_sm,
+    mask_hbm,
+    noise_hbm,
+    live_hbm,
     w_hbm,
     g_hbm,
     out_ref,
@@ -79,6 +81,9 @@
     gath,
     wt,
     gate,
+    mask_sm,
+    noise_sm,
+    live_sm,
     loc,
     dds,
     ddr,
@@ -113,8 +118,8 @@
     FP = FG // half
     CB = T // half
     GR = math.gcd(FP, HD)
-    QB = mask_sm.shape[1]
-    NB = mask_sm.shape[2]
+    QB = mask_hbm.shape[1]
+    NB = mask_hbm.shape[2]
 
     e = lax.axis_index("stretch")
     t = lax.axis_index("tp")
@@ -153,7 +158,11 @@
     ld_f = pltpu.make_async_copy(s_hbm, fx.at[:, pl.ds(e * R, R), :], loc.at[3])
     ld_w = pltpu.make_async_copy(w_hbm, wt, loc.at[4])
     ld_g = pltpu.make_async_copy(g_hbm, gate, loc.at[5])
-    for copy in ld_q + [ld_f, ld_hist, ld_w, ld_g]:
+    scalars = 9 + 2 * HH
+    ld_mask = pltpu.make_async_copy(mask_hbm, mask_sm, loc.at[scalars])
+    ld_noise = pltpu.make_async_copy(noise_hbm, noise_sm, loc.at[scalars + 1])
+    ld_live = pltpu.make_async_copy(live_hbm, live_sm, loc.at[scalars + 2])
+    for copy in ld_q + [ld_f, ld_mask, ld_noise, ld_live, ld_hist, ld_w, ld_g]:
         copy.start()
 
     barrier = pltpu.get_barrier_semaphore()
@@ -163,6 +172,8 @@
     for device in (at(a2, b2), other_core):
         pl.semaphore_signal(barrier, inc=1, device_id=device, device_id_type=MESH)
 
+    for copy in (ld_mask, ld_noise, ld_live):
+        copy.wait()
     lane = lax.broadcasted_iota(jnp.int32, (1, T), 1)
     swapped = ((lane // R) % S) * (S * R) + (lane // (S * R)) * R + lane % R
     own_order = jnp.where(e == 0, lane, swapped) // BLK
@@ -260,8 +271,9 @@
         q1_copy(k).start()
     q1_own.start()
     ld_hist.wait()
-    for p in (3, 1, 2):
-        kv_copy(0, p).start()
+    for h in range(HH):
+        for p in (3, 1, 2):
+            kv_copy(h, p).start()
     df.wait_recv()
     for p in (3, 1, 2):
         f_copy(p).start()
@@ -272,9 +284,6 @@
     for k in range(1, S):
         q1_copy(k).wait_recv()
     for h in range(HH):
-        if h > 0:
-            for p in (3, 1, 2):
-                kv_copy(h, p).start()
         for k in (4, 3, 5, 2, 6, 1, 7) if S == 8 else range(1, S):
             q2_copy(h, k).start()
         q2_own(h).start()
@@ -305,17 +314,9 @@
         for k in range(1, S):
             q2_copy(h, k).wait_recv()
 
-        def chunk(n, carry):
-            k = (n + 1) % half
+        def score(k):
             cols = pl.ds(pl.multiple_of(((ia + k) % half) * CB, CB), CB)
             queries = jnp.concatenate([q[h, 0, cols, :], q[h, 1, cols, :]], axis=0)
-            scores = []
-            for p in range(4):
-                first = tp_of(*block[p]) * HR
-                part = dot(kv[h, p, 0], queries, 1, 1)
-                for r in range(HR // BLK):
-                    bias = jnp.where(first + r * BLK < live, 0.0, NEGATIVE)
-                    scores.append(part[r * BLK : (r + 1) * BLK] + bias)
             fresh_bias = []
             for p in range(4):
                 u = (tp_of(*block[p]) * R) // BLK
@@ -327,23 +328,38 @@
                     row = jnp.concatenate([left, right], axis=1)
                     fresh_bias.append(jnp.broadcast_to(row, (R, 2 * CB)))
             fresh = dot(frb[0, :, h_cols(h)], queries, 1, 1) + jnp.concatenate(fresh_bias, axis=0)
-            peak = jnp.max(fresh, axis=0, keepdims=True)
-            for part in scores:
-                peak = jnp.maximum(peak, jnp.max(part, axis=0, keepdims=True))
-            weights = jnp.exp2((fresh - peak) * EXP2_SCALE)
+            scores = [fresh]
+            for p in range(4):
+                part = dot(kv[h, p, 0], queries, 1, 1)
+                scores += [part[r * BLK : (r + 1) * BLK] for r in range(HR // BLK)]
+            return scores
+
+        per = HR // BLK
+        alive = [
+            tp_of(*block[p]) * HR + r * BLK < live for p in range(4) for r in range(per)
+        ]
+
+        def attend(k, scores):
+            peak = jnp.max(scores[0], axis=0, keepdims=True)
+            for part, on in zip(scores[1:], alive):
+                top = jnp.max(part, axis=0, keepdims=True)
+                peak = jnp.maximum(peak, jnp.where(on, top, NEGATIVE))
+            weights = jnp.exp2(
+                (scores[0] - jnp.where(peak > 0.5 * NEGATIVE, peak, -NEGATIVE)) * EXP2_SCALE
+            )
             total = jnp.sum(weights, axis=0, keepdims=True)
             output = dot(frb[1, :, h_cols(h)], weights.astype(BF16), 0, 0)
-            per = HR // BLK
             for p in range(4):
                 block_weights = []
-                for part in scores[p * per : (p + 1) * per]:
-                    weights = jnp.exp2((part - peak) * EXP2_SCALE)
+                for r in range(per):
+                    shift = jnp.where(alive[p * per + r], peak, -NEGATIVE)
+                    weights = jnp.exp2((scores[1 + p * per + r] - shift) * EXP2_SCALE)
                     total = total + jnp.sum(weights, axis=0, keepdims=True)
                     block_weights.append(weights.astype(BF16))
                 output = output + dot(
                     kv[h, p, 1], jnp.concatenate(block_weights, axis=0), 0, 0
                 )
-            output = (output / total).astype(BF16)
+            output = (output / jnp.maximum(total, SMALL)).astype(BF16)
             obuf[h, k, 0] = output[:, :CB]
             obuf[h, k, 1] = output[:, CB:]
             stats[h, k] = jnp.concatenate(
@@ -351,14 +367,21 @@
                 axis=0,
             )
 
-            @pl.when(n >= 1)
-            def _():
-                o_copy(h, n).start()
-                os_copy(h, n).start()
+        def chunks(m, carry):
+            ks = [(m * STEP + n + 1) % half for n in range(STEP)]
+            all_scores = [score(k) for k in ks]
+            for k, scores in zip(ks, all_scores):
+                attend(k, scores)
+            for k in ks:
+
+                @pl.when(k > 0)
+                def _():
+                    o_copy(h, k).start()
+                    os_copy(h, k).start()
 
             return carry
 
-        return lax.fori_loop(0, half, chunk, carry)
+        return lax.fori_loop(0, half // STEP, chunks, carry)
 
     lax.fori_loop(0, HH, head, 0)
 
@@ -413,47 +436,53 @@
             _, _, output = merged(parts)
             fin[c, p * GR : (p + 1) * GR, :] = output.astype(BF16)
 
-    gd = remote(fin.at[1 - e], gath.at[1, a, b], dds.at[3], ddr.at[3], other_core)
+    gd = remote(fin.at[1 - e], gath.at[b, a, 1], dds.at[3], ddr.at[3], other_core)
     gd.start()
-    g_own = pltpu.make_async_copy(fin.at[e], gath.at[0, a, b], loc.at[8 + 2 * HH])
+    g_own = pltpu.make_async_copy(fin.at[e], gath.at[a, b, 0], loc.at[8 + 2 * HH])
     g_own.start()
 
     def g1_copy(kind, k):
-        dst = gath.at[0, a, b] if kind == 0 else gath.at[1, b, a]
-        src = fin.at[e] if kind == 0 else gath.at[1, b, a]
+        dst = gath.at[a, b, kind]
+        src = fin.at[e] if kind == 0 else dst
         return remote(src, dst, g1s.at[kind, k], g1r.at[kind, k], at((a + k) % S, b))
 
-    for k in range(1, S):
+    arrivals = [0] + [k for d in range(1, half) for k in (d, S - d)] + [half]
+    for k in arrivals[1:]:
         g1_copy(0, k).start()
     gd.wait_recv()
-    for k in range(1, S):
+    for k in arrivals[1:]:
         g1_copy(1, k).start()
     g_own.wait()
 
-    def g2_copy(d, s, kind):
+    def g2_copy(d, s, k):
         sign = 1 - 2 * d
-        source = (b + S - sign * (s - 1)) % S
-        slab = gath.at[0, :, source] if kind == 0 else gath.at[1, source]
-        return remote(
-            slab, slab, g2s.at[d, s, kind], g2r.at[d, s, kind], at(a, (b + S + sign) % S)
-        )
-
-    sent = []
-    for s in range(1, half + 1):
-        for kind in range(2):
-            if s == 1:
-                for k in range(1, S):
-                    g1_copy(kind, k).wait_recv()
-            for d in range(2):
-                if s == half and kind != d:
-                    continue
-                if s > 1:
-                    g2_copy(d, s - 1, kind).wait_recv()
-                g2_copy(d, s, kind).start()
-                sent.append((d, s, kind))
-    for d in range(2):
-        g2_copy(d, half - 1, 1 - d).wait_recv()
-        g2_copy(d, half, d).wait_recv()
+        piece = gath.at[(a + S - k) % S, (b + S - sign * (s - 1)) % S]
+        return remote(
+            piece,
+            piece,
+            g2s.at[d, s - 1, k],
+            g2r.at[d, s - 1, k],
+            at(a, (b + S + sign) % S),
+        )
+
+    sends = [
+        (place + S * (s - 1), s, d, k)
+        for place, k in enumerate(arrivals)
+        for s in range(1, half + 1)
+        for d in range(2)
+        if s < half or place % 2 == d
+    ]
+    sends = [key[1:] for key in sorted(sends)]
+    for s, d, k in sends:
+        if s == 1 and d == 0 and k > 0:
+            g1_copy(0, k).wait_recv()
+            g1_copy(1, k).wait_recv()
+        if s > 1:
+            g2_copy(d, s - 1, k).wait_recv()
+        g2_copy(d, s, k).start()
+    for s, d, k in sends:
+        if (s + 1, d, k) not in sends:
+            g2_copy(d, s, k).wait_recv()
 
     ld_w.wait()
     ld_g.wait()
@@ -468,7 +497,13 @@
                 rows = jnp.concatenate(
                     [
                         jnp.concatenate(
-                            [gath[kind, 2 * i + pa, 2 * j + pb] for j in range(half)], axis=0
+                            [
+                                gath[2 * i + pa, 2 * j + pb, 0]
+                                if kind == 0
+                                else gath[2 * j + pb, 2 * i + pa, 1]
+                                for j in range(half)
+                            ],
+                            axis=0,
                         )
                         for i in range(half)
                     ],
@@ -497,12 +532,10 @@
     gate_column = jnp.sum(jnp.where(levels == noise_sm[0], gate[...], 0.0), axis=1, keepdims=True)
     out_ref[...] = ((natural + crossed) * gate_column).astype(BF16)
 
-    for copy in (dq, df, dm, gd):
+    for copy in (dq, df, dm):
         copy.wait_send()
     for k in range(1, S):
         q1_copy(k).wait_send()
-        g1_copy(0, k).wait_send()
-        g1_copy(1, k).wait_send()
     for p in (1, 2, 3):
         f_copy(p).wait_send()
     for h in range(HH):
@@ -510,14 +543,19 @@
             kv_copy(h, p).wait_send()
         for k in range(1, S):
             q2_copy(h, k).wait_send()
+    for h in range(HH):
         for k in range(1, half):
             o_copy(h, k).wait_send()
             os_copy(h, k).wait_send()
     for k in range(1, half):
         b_copy(k).wait_send()
         bs_copy(k).wait_send()
-    for key in sent:
-        g2_copy(*key).wait_send()
+    gd.wait_send()
+    for k in range(1, S):
+        g1_copy(0, k).wait_send()
+        g1_copy(1, k).wait_send()
+    for s, d, k in sends:
+        g2_copy(d, s, k).wait_send()
 
 
 def on_device(
@@ -534,12 +572,11 @@
     CB = T // half
     C = out_weight.shape[1]
     DMA = pltpu.SemaphoreType.DMA
-    any_space = pl.BlockSpec(memory_space=pl.ANY)
-    smem = pl.BlockSpec(memory_space=pltpu.SMEM)
+    any_space = pl.BlockSpec(memory_space=pltpu.HBM)
     out = pl.pallas_call(
         functools.partial(kernel, side),
         out_shape=jax.ShapeDtypeStruct((C, T), BF16),
-        in_specs=[any_space, any_space, any_space, smem, smem, smem, any_space, any_space],
+        in_specs=[any_space] * 8,
         out_specs=pl.BlockSpec(memory_space=pltpu.VMEM),
         scratch_shapes=[
             pltpu.VMEM((2, HR, F), BF16),
@@ -559,10 +596,13 @@
             pltpu.VMEM((half, 2, FP, CB), BF16),
             pltpu.VMEM((half, 4 * HH, 1, CB), F32),
             pltpu.VMEM((2, FP, CB), BF16),
-            pltpu.VMEM((2, S, S, FP, CB), BF16),
+            pltpu.VMEM((S, S, 2, FP, CB), BF16),
             pltpu.VMEM((C, F), BF16),
             pltpu.VMEM((C, gate_table.shape[0]), F32),
-            DMA((9 + 2 * HH,)),
+            pltpu.SMEM(block_mask.shape, jnp.int32),
+            pltpu.SMEM(noise_level.shape, jnp.int32),
+            pltpu.SMEM(history_blocks.shape, jnp.int32),
+            DMA((12 + 2 * HH,)),
             DMA((4,)),
             DMA((4,)),
             DMA((S,)),
@@ -583,11 +623,11 @@
             DMA((half,)),
             DMA((2, S)),
             DMA((2, S)),
-            DMA((2, half + 1, 2)),
-            DMA((2, half + 1, 2)),
+            DMA((2, half, S)),
+            DMA((2, half, S)),
         ],
         compiler_params=pltpu.CompilerParams(
-            collective_id=0, has_side_effects=True, vmem_limit_bytes=48 * 1024 * 1024
+            collective_id=0, has_side_effects=True, vmem_limit_bytes=63 * 1024 * 1024
         ),
     )(
         query[0],

time: 105 us -> 95.4 us (0.909)
  local copies, waits for them, and re-layouts: 6.96 us -> 1.54 us
  Pallas kernels: 96.4 us -> 92.4 us
    unnamed x13 -> x1, local copies, waits for them, and re-layouts: 6.96 us -> 1.54 us
    pallas_call x1, Pallas kernels: 96.4 us -> 92.4 us  [on_device(): pl.pallas_call(functools.partial(kernel, side), out_shape=jax.ShapeDtypeS...]
where the time goes in v2:
time: 95.4 us; the launch traced here: 95.2 us
  Pallas kernels  92.4 us (97%)
  local copies, waits for them, and re-layouts  1.54 us (2%)
  between operations  1.3 us (1%)
    pallas_call x1, Pallas kernels, on_device(): pl.pallas_call(functools.partial(kernel, side), out_shape=jax.ShapeDtypeS...  92.4 us

profile of v2, /device:TPU:513, one launch (start us, length us, event | category | flops | bytes accessed | tf_op | source)
XLA Modules:
  0.0 95.2 jit_solution(12329309651928921276)
XLA Ops:
  1.3 92.4 %shard_map.82 = bf16[96,512]{1,0:T(8,128)(2,1)} custom-call(bf16[8,3072]{1,0:T(8,128)(2,1)} %bitcast.11, bf16[2,8,3072]{2,1,0:T(8,128)(2,1)} %bitcast.10, bf16[2,256,3072]{2,1,0:T(8,128)(2,1)} %h_hbm.1, s32[1,4,8]{2,1,0:T(4,128)} %mask_hbm.1, s32[1]{0:T(128)S(6)} %copy.10.noise_hbm, s32[1]{0:T(128)S(6)} %copy.11.live_hbm, bf16[96,3072]{1,0:T(8,128)(2,1)} %bitcast.7, ...), custom_call_target="tpu_custom_call" | custom-call | tf_op jit(solution)/shard_map/pallas_call | solution.py:576
  93.7 1.5 %copy.12 = bf16[1,512,96]{1,2,0:T(8,128)(2,1)} copy(bf16[1,512,96]{1,2,0:T(8,128)(2,1)} %bitcast.9) | data formatting | bytes 196608

commit v3 on v2

--- a/solution.py
+++ b/solution.py
@@ -134,6 +134,9 @@
     def at(a_, b_):
         return {"tp": tp_of(a_, b_)}
 
+    def across(a_, b_):
+        return {"stretch": 1 - e, "tp": tp_of(a_, b_)}
+
     other_core = {"stretch": 1 - e}
 
     def group_of(a_, b_):
@@ -151,7 +154,7 @@
     ld_hist = pltpu.make_async_copy(h_hbm, hist, loc.at[0])
     ld_q = [
         pltpu.make_async_copy(
-            q_hbm.at[:, pl.ds(p * (F // 2), F // 2)], qx.at[p, e], loc.at[1 + p]
+            q_hbm.at[:, pl.ds(p * (F // 2), F // 2)], qx.at[p], loc.at[1 + p]
         )
         for p in range(2)
     ]
@@ -165,9 +168,16 @@
     for copy in ld_q + [ld_f, ld_mask, ld_noise, ld_live, ld_hist, ld_w, ld_g]:
         copy.start()
 
+    nearest = [0] + [k for d in range(1, half) for k in (d, S - d)] + [half]
+
     barrier = pltpu.get_barrier_semaphore()
     for k in range(1, S):
-        for device in (at((a + k) % S, b), at(a, (b + k) % S)):
+        for device in (
+            at((a + k) % S, b),
+            at(a, (b + k) % S),
+            across((a + k) % S, b),
+            across(a, (b + k) % S),
+        ):
             pl.semaphore_signal(barrier, inc=1, device_id=device, device_id_type=MESH)
     for device in (at(a2, b2), other_core):
         pl.semaphore_signal(barrier, inc=1, device_id=device, device_id_type=MESH)
@@ -190,9 +200,8 @@
 
     for copy in ld_q + [ld_f]:
         copy.wait()
-    pl.semaphore_wait(barrier, 2 * (S - 1) + 2)
-
-    dq = remote(qx.at[:, e], qx.at[:, e], dds.at[0], ddr.at[0], other_core)
+    pl.semaphore_wait(barrier, 4 * (S - 1) + 2)
+
     df = remote(
         fx.at[:, pl.ds(e * R, R), :],
         fx.at[:, pl.ds(e * R, R), :],
@@ -201,22 +210,36 @@
         other_core,
     )
     dm = remote(msend, mtab.at[e], dds.at[2], ddr.at[2], other_core)
-    dq.start()
     df.start()
     dm.start()
 
-    def q_cols(b_):
-        return pl.ds(pl.multiple_of(((b_ % 2) * 2 + e) * FG, FG), FG)
-
-    q1_rows = pl.ds(pl.multiple_of(b * R, R), R)
+    def q_cols(b_, core):
+        return pl.ds(pl.multiple_of(((b_ % 2) * 2 + core) * FG, FG), FG)
+
+    def q1_rows(b_):
+        return pl.ds(pl.multiple_of(b_ * R, R), R)
 
     def q1_copy(k):
         b_ = (b + k) % S
         return remote(
-            qx.at[:, :, :, q_cols(b_)], q1.at[:, :, q1_rows, :], q1s.at[k], q1r.at[k], at(a, b_)
-        )
-
-    q1_own = pltpu.make_async_copy(qx.at[:, :, :, q_cols(b)], q1.at[:, :, q1_rows, :], loc.at[6])
+            qx.at[:, :, q_cols(b_, e)],
+            q1.at[:, e, q1_rows(b), :],
+            q1s.at[0, k],
+            q1r.at[0, k],
+            at(a, b_),
+        )
+
+    def q1_across(k):
+        a_ = (a + k) % S
+        return remote(
+            qx.at[:, :, q_cols(a_, 1 - e)],
+            q1.at[:, e, q1_rows(a), :],
+            q1s.at[1, k],
+            q1r.at[1, k],
+            across(a_, b),
+        )
+
+    q1_own = pltpu.make_async_copy(qx.at[:, :, q_cols(b, e)], q1.at[:, e, q1_rows(b), :], loc.at[6])
 
     def kv_cols(p, h):
         start = group_of(*block[p]) * FG + h * HD
@@ -266,14 +289,14 @@
             q1.at[a % 2, :, :, h_cols(h)], q.at[h, :, q_rows, :], loc.at[8 + HH + h]
         )
 
-    dq.wait_recv()
     for k in range(1, S):
         q1_copy(k).start()
+        q1_across(k).start()
+    q1_across(0).start()
     q1_own.start()
     ld_hist.wait()
-    for h in range(HH):
-        for p in (3, 1, 2):
-            kv_copy(h, p).start()
+    for p in (3, 1, 2):
+        kv_copy(0, p).start()
     df.wait_recv()
     for p in (3, 1, 2):
         f_copy(p).start()
@@ -281,10 +304,15 @@
         kv_own(h).start()
     f_own.start()
     q1_own.wait()
-    for k in range(1, S):
-        q1_copy(k).wait_recv()
+    for k in range(S):
+        q1_across(k).wait_recv()
+        if k > 0:
+            q1_copy(k).wait_recv()
     for h in range(HH):
-        for k in (4, 3, 5, 2, 6, 1, 7) if S == 8 else range(1, S):
+        if h > 0:
+            for p in (3, 1, 2):
+                kv_copy(h, p).start()
+        for k in reversed(nearest[1:]):
             q2_copy(h, k).start()
         q2_own(h).start()
 
@@ -436,23 +464,26 @@
             _, _, output = merged(parts)
             fin[c, p * GR : (p + 1) * GR, :] = output.astype(BF16)
 
-    gd = remote(fin.at[1 - e], gath.at[b, a, 1], dds.at[3], ddr.at[3], other_core)
-    gd.start()
     g_own = pltpu.make_async_copy(fin.at[e], gath.at[a, b, 0], loc.at[8 + 2 * HH])
     g_own.start()
 
-    def g1_copy(kind, k):
-        dst = gath.at[a, b, kind]
-        src = fin.at[e] if kind == 0 else dst
-        return remote(src, dst, g1s.at[kind, k], g1r.at[kind, k], at((a + k) % S, b))
-
-    arrivals = [0] + [k for d in range(1, half) for k in (d, S - d)] + [half]
-    for k in arrivals[1:]:
-        g1_copy(0, k).start()
-    gd.wait_recv()
-    for k in arrivals[1:]:
-        g1_copy(1, k).start()
+    def g1_copy(k):
+        return remote(
+            fin.at[e], gath.at[a, b, 0], g1s.at[0, k], g1r.at[0, k], at((a + k) % S, b)
+        )
+
+    def g1_across(k):
+        return remote(
+            fin.at[1 - e], gath.at[b, a, 1], g1s.at[1, k], g1r.at[1, k], across(a, (b + k) % S)
+        )
+
+    arrivals = nearest
+    for k in arrivals:
+        g1_across(k).start()
+        if k > 0:
+            g1_copy(k).start()
     g_own.wait()
+    g1_across(0).wait_recv()
 
     def g2_copy(d, s, k):
         sign = 1 - 2 * d
@@ -475,8 +506,8 @@
     sends = [key[1:] for key in sorted(sends)]
     for s, d, k in sends:
         if s == 1 and d == 0 and k > 0:
-            g1_copy(0, k).wait_recv()
-            g1_copy(1, k).wait_recv()
+            g1_copy(k).wait_recv()
+            g1_across(k).wait_recv()
         if s > 1:
             g2_copy(d, s - 1, k).wait_recv()
         g2_copy(d, s, k).start()
@@ -532,10 +563,12 @@
     gate_column = jnp.sum(jnp.where(levels == noise_sm[0], gate[...], 0.0), axis=1, keepdims=True)
     out_ref[...] = ((natural + crossed) * gate_column).astype(BF16)
 
-    for copy in (dq, df, dm):
+    for copy in (df, dm):
         copy.wait_send()
-    for k in range(1, S):
-        q1_copy(k).wait_send()
+    for k in range(S):
+        q1_across(k).wait_send()
+        if k > 0:
+            q1_copy(k).wait_send()
     for p in (1, 2, 3):
         f_copy(p).wait_send()
     for h in range(HH):
@@ -550,10 +583,10 @@
     for k in range(1, half):
         b_copy(k).wait_send()
         bs_copy(k).wait_send()
-    gd.wait_send()
-    for k in range(1, S):
-        g1_copy(0, k).wait_send()
-        g1_copy(1, k).wait_send()
+    for k in range(S):
+        g1_across(k).wait_send()
+        if k > 0:
+            g1_copy(k).wait_send()
     for s, d, k in sends:
         g2_copy(d, s, k).wait_send()
 
@@ -580,7 +613,7 @@
         out_specs=pl.BlockSpec(memory_space=pltpu.VMEM),
         scratch_shapes=[
             pltpu.VMEM((2, HR, F), BF16),
-            pltpu.VMEM((2, 2, R, F // 2), BF16),
+            pltpu.VMEM((2, R, F // 2), BF16),
             pltpu.VMEM((2, 2 * R, F), BF16),
             pltpu.VMEM((block_mask.shape[2], 1, T), F32),
             pltpu.VMEM((2, block_mask.shape[2], 1, T), F32),
@@ -605,8 +638,8 @@
             DMA((12 + 2 * HH,)),
             DMA((4,)),
             DMA((4,)),
-            DMA((S,)),
-            DMA((S,)),
+            DMA((2, S)),
+            DMA((2, S)),
             DMA((HH, S)),
             DMA((HH, S)),
             DMA((HH, 4)),

time: 95.4 us -> 90.7 us (0.951)
  Pallas kernels: 92.4 us -> 87.2 us
    pallas_call x1, Pallas kernels: 92.4 us -> 87.2 us  [on_device(): pl.pallas_call(functools.partial(kernel, side), out_shape=jax.ShapeDtypeS...]
where the time goes in v3:
time: 90.7 us; the launch traced here: 90.1 us
  Pallas kernels  87.2 us (96%)
  local copies, waits for them, and re-layouts  1.54 us (2%)
  between operations  1.3 us (1%)
    pallas_call x1, Pallas kernels, on_device(): pl.pallas_call(functools.partial(kernel, side), out_shape=jax.ShapeDtypeS...  87.2 us

profile of v3, /device:TPU:513, one launch (start us, length us, event | category | flops | bytes accessed | tf_op | source)
XLA Modules:
  0.0 90.1 jit_solution(14330179202369272093)
XLA Ops:
  1.3 87.2 %shard_map.82 = bf16[96,512]{1,0:T(8,128)(2,1)} custom-call(bf16[8,3072]{1,0:T(8,128)(2,1)} %bitcast.11, bf16[2,8,3072]{2,1,0:T(8,128)(2,1)} %bitcast.10, bf16[2,256,3072]{2,1,0:T(8,128)(2,1)} %h_hbm.1, s32[1,4,8]{2,1,0:T(4,128)} %mask_hbm.1, s32[1]{0:T(128)S(6)} %copy.10.noise_hbm, s32[1]{0:T(128)S(6)} %copy.11.live_hbm, bf16[96,3072]{1,0:T(8,128)(2,1)} %bitcast.7, ...), custom_call_target="tpu_custom_call" | custom-call | tf_op jit(solution)/shard_map/pallas_call | solution.py:609
  88.5 1.5 %copy.12 = bf16[1,512,96]{1,2,0:T(8,128)(2,1)} copy(bf16[1,512,96]{1,2,0:T(8,128)(2,1)} %bitcast.9) | data formatting | bytes 196608

commit v4 on v3

--- a/solution.py
+++ b/solution.py
@@ -289,7 +289,7 @@
             q1.at[a % 2, :, :, h_cols(h)], q.at[h, :, q_rows, :], loc.at[8 + HH + h]
         )
 
-    for k in range(1, S):
+    for k in reversed(nearest[1:]):
         q1_copy(k).start()
         q1_across(k).start()
     q1_across(0).start()
@@ -446,6 +446,26 @@
     for k in range(1, half):
         bs_copy(k).start()
         b_copy(k).start()
+    for copy in (df, dm):
+        copy.wait_send()
+    for k in range(S):
+        q1_across(k).wait_send()
+        if k > 0:
+            q1_copy(k).wait_send()
+    for p in (1, 2, 3):
+        f_copy(p).wait_send()
+    for h in range(HH):
+        for p in (1, 2, 3):
+            kv_copy(h, p).wait_send()
+        for k in range(1, S):
+            q2_copy(h, k).wait_send()
+    for h in range(HH):
+        for k in range(1, half):
+            o_copy(h, k).wait_send()
+            os_copy(h, k).wait_send()
+    ld_g.wait()
+    levels = lax.broadcasted_iota(jnp.int32, gate.shape, 1)
+    gate_column = jnp.sum(jnp.where(levels == noise_sm[0], gate[...], 0.0), axis=1, keepdims=True)
     for k in range(1, half):
         bs_copy(k).wait_recv()
         b_copy(k).wait_recv()
@@ -511,12 +531,20 @@
         if s > 1:
             g2_copy(d, s - 1, k).wait_recv()
         g2_copy(d, s, k).start()
+    for k in range(1, half):
+        b_copy(k).wait_send()
+        bs_copy(k).wait_send()
+    for k in range(S):
+        g1_across(k).wait_send()
+        if k > 0:
+            g1_copy(k).wait_send()
+    for s, d, k in sends:
+        g2_copy(d, s, k).wait_send()
     for s, d, k in sends:
         if (s + 1, d, k) not in sends:
             g2_copy(d, s, k).wait_recv()
 
     ld_w.wait()
-    ld_g.wait()
     results = []
     for kind in range(2):
         e_kind = e if kind == 0 else 1 - e
@@ -559,36 +587,7 @@
         axis=0,
     )
     crossed = crossed.T[:width]
-    levels = lax.broadcasted_iota(jnp.int32, gate.shape, 1)
-    gate_column = jnp.sum(jnp.where(levels == noise_sm[0], gate[...], 0.0), axis=1, keepdims=True)
     out_ref[...] = ((natural + crossed) * gate_column).astype(BF16)
-
-    for copy in (df, dm):
-        copy.wait_send()
-    for k in range(S):
-        q1_across(k).wait_send()
-        if k > 0:
-            q1_copy(k).wait_send()
-    for p in (1, 2, 3):
-        f_copy(p).wait_send()
-    for h in range(HH):
-        for p in (1, 2, 3):
-            kv_copy(h, p).wait_send()
-        for k in range(1, S):
-            q2_copy(h, k).wait_send()
-    for h in range(HH):
-        for k in range(1, half):
-            o_copy(h, k).wait_send()
-            os_copy(h, k).wait_send()
-    for k in range(1, half):
-        b_copy(k).wait_send()
-        bs_copy(k).wait_send()
-    for k in range(S):
-        g1_across(k).wait_send()
-        if k > 0:
-            g1_copy(k).wait_send()
-    for s, d, k in sends:
-        g2_copy(d, s, k).wait_send()
 
 
 def on_device(

time: 90.7 us -> 90.6 us (level)
  no operation moved by 1% of the time
where the time goes in v4:
time: 90.6 us; the launch traced here: 89.5 us
  Pallas kernels  86.6 us (96%)
  local copies, waits for them, and re-layouts  1.54 us (2%)
  between operations  1.3 us (1%)
    pallas_call x1, Pallas kernels, on_device(): pl.pallas_call(functools.partial(kernel, side), out_shape=jax.ShapeDtypeS...  86.6 us

profile of v4, /device:TPU:513, one launch (start us, length us, event | category | flops | bytes accessed | tf_op | source)
XLA Modules:
  0.0 89.5 jit_solution(1793450534834031485)
XLA Ops:
  1.3 86.6 %shard_map.82 = bf16[96,512]{1,0:T(8,128)(2,1)} custom-call(bf16[8,3072]{1,0:T(8,128)(2,1)} %bitcast.11, bf16[2,8,3072]{2,1,0:T(8,128)(2,1)} %bitcast.10, bf16[2,256,3072]{2,1,0:T(8,128)(2,1)} %h_hbm.1, s32[1,4,8]{2,1,0:T(4,128)} %mask_hbm.1, s32[1]{0:T(128)S(6)} %copy.10.noise_hbm, s32[1]{0:T(128)S(6)} %copy.11.live_hbm, bf16[96,3072]{1,0:T(8,128)(2,1)} %bitcast.7, ...), custom_call_target="tpu_custom_call" | custom-call | tf_op jit(solution)/shard_map/pallas_call | solution.py:608
  87.9 1.5 %copy.12 = bf16[1,512,96]{1,2,0:T(8,128)(2,1)} copy(bf16[1,512,96]{1,2,0:T(8,128)(2,1)} %bitcast.9) | data formatting | bytes 196608
